TPU v7x, 32 devices: a whole 2x2x4 slice. The times are simulated.
32 devices in a mesh: ka: 8 (over y, x, core), ga: 4 (over z).
Axes of the slice: x: 2, y: 2, z: 4, core: 2. Of those that a mesh axis runs over, the one named last changes fastest.
Arguments:
- coeffs: bfloat16 [8, 2, 7680, 256], P('ka', None, 'ga'), may hold values from -1 to 1
- projectors: bfloat16 [2, 7680, 1024], P(None, 'ga'), may hold values from -1.5 to 1.5
- proj_deriv: bfloat16 [2, 7680, 1024], P(None, 'ga'), may hold values from -1.5 to 1.5
- shift_map: int32 [7680], P('ga'), may hold values from 0 to 7679, as said below
- atom_of: int32 [1024], replicated, may hold values from 0 to 127, as said below
Outputs:
- transport: float32 [8, 2, 256, 256], P('ka')
- forces: float32 [128], replicated
Inputs may be any that keep to these rules, and one draw needn't show every extreme that they name: `shift_map`: a permutation that maps each aligned block of 1920 plane waves onto itself. `atom_of`: each atom owns exactly 8 projectors.
All inputs are finite; a program needn't handle non-finite values.
Results may differ from a plain program's by a relative error of at most 0.0003.
Values may be sent and summed in bfloat16 or wider, within the bound.
A program may use at most 128 MiB of HBM per device.

v0:
```python
import jax
import jax.numpy as jnp
from jax import lax
from jax.sharding import PartitionSpec as P

NA = 128
NEWTON = 2


def from_behind(block, axis, distance):
    devices = range(lax.axis_size(axis))
    route = [((i - distance) % len(devices), i) for i in devices]
    return lax.ppermute(block, axis, route)


def cmul(left, right):
    highest = lax.Precision.HIGHEST
    left_re, left_im = (left[..., 0, :, :], left[..., 1, :, :])
    right_re, right_im = (right[..., 0, :, :], right[..., 1, :, :])
    real_part = jnp.matmul(left_re, right_re, precision=highest) - jnp.matmul(
        left_im, right_im, precision=highest
    )
    imag_part = jnp.matmul(left_re, right_im, precision=highest) + jnp.matmul(
        left_im, right_re, precision=highest
    )
    return jnp.stack([real_part, imag_part], axis=-3)


def invert(intersection, eye_c):
    estimate = jnp.broadcast_to(eye_c, intersection.shape)
    for newton_step in range(NEWTON):
        estimate = cmul(estimate, 2.0 * eye_c - cmul(intersection, estimate))
    return estimate


def project(proj_table, columns, swapped):
    real_part = jnp.einsum("gp,kgn->kpn", proj_table, columns, preferred_element_type=jnp.float32)
    imag_part = jnp.einsum("gp,kgn->kpn", proj_table, swapped, preferred_element_type=jnp.float32)
    return jnp.stack([real_part, imag_part], axis=1)


def local(coeffs, projectors, proj_deriv, shift_map, atom_of):
    points_here = coeffs.shape[0]
    plane_rows = coeffs.shape[2]
    bands = coeffs.shape[3]
    string_devices = lax.axis_size("ka")
    position = lax.axis_index("ka")
    total_points = points_here * string_devices
    eye_c = jnp.stack([jnp.eye(bands, dtype=jnp.float32), jnp.zeros((bands, bands), jnp.float32)])
    arrived = from_behind(coeffs[0], "ka", -1)
    local_map = shift_map % plane_rows
    wrapped = jnp.where(position == string_devices - 1, arrived[:, local_map, :], arrived)
    following = jnp.concatenate([coeffs[1:], wrapped[None]], axis=0)
    columns = coeffs.reshape(points_here, 2 * plane_rows, bands)
    own_swap = jnp.concatenate([coeffs[:, 1], -coeffs[:, 0]], axis=1)
    next_cols = following.reshape(points_here, 2 * plane_rows, bands)
    next_swap = jnp.concatenate([following[:, 1], -following[:, 0]], axis=1)
    batch_dims = (((1,), (1,)), ((0,), (0,)))
    intersection_part = jnp.stack(
        [
            lax.dot_general(columns, next_cols, batch_dims, preferred_element_type=jnp.float32),
            lax.dot_general(columns, next_swap, batch_dims, preferred_element_type=jnp.float32),
        ],
        axis=1,
    )
    proj_table = projectors.reshape(2 * plane_rows, projectors.shape[2])
    deriv_table = proj_deriv.reshape(2 * plane_rows, proj_deriv.shape[2])
    proj_part = project(proj_table, columns, own_swap)
    deriv_part = project(deriv_table, columns, own_swap)
    intersections = lax.psum(intersection_part, "ga")
    proj_vals, deriv_vals = (
        lax.psum_scatter(proj_part, "ga", scatter_dimension=2, tiled=True),
        lax.psum_scatter(deriv_part, "ga", scatter_dimension=2, tiled=True),
    )
    share_rows = proj_vals.shape[2]
    atom_ids = lax.dynamic_slice_in_dim(atom_of, lax.axis_index("ga") * share_rows, share_rows, 0)
    inverses = invert(intersections, eye_c)
    chain_list = [inverses[0]]
    local_chain = jnp.stack(chain_list)
    device_product = chain_list[-1]
    everyone = lax.all_gather(device_product[None], "ka", axis=0, tiled=True)

    def advance(running, element):
        number, matrix = element
        return (jnp.where(number < position, cmul(running, matrix), running), None)

    offset, unused = lax.scan(
        advance, eye_c, (jnp.arange(string_devices, dtype=jnp.int32), everyone)
    )
    transport = cmul(offset[None], local_chain)
    weighted = cmul(proj_vals, transport)
    per_proj = (
        jnp.sum(deriv_vals[:, 0] * weighted[:, 1] - deriv_vals[:, 1] * weighted[:, 0], axis=(0, 2))
        / total_points
    )
    onehot = (atom_ids[None, :] == jnp.arange(NA, dtype=jnp.int32)[:, None]).astype(jnp.float32)
    force_part = jnp.dot(onehot, per_proj, precision=lax.Precision.HIGHEST)
    forces = lax.psum(force_part, ("ka", "ga"))
    return (transport, forces)


def solution(mesh):
    placed = (P("ka", None, "ga", None), P(None, "ga", None), P(None, "ga", None), P("ga"), P())
    return jax.shard_map(
        local,
        mesh=mesh,
        in_specs=placed,
        out_specs=(P("ka", None, None, None), P()),
        check_vma=False,
    )
```

profile of v0, /device:TPU:0, one launch (start us, length us, event | category | flops | bytes accessed | tf_op | source)
XLA Modules:
  0.0 296.8 jit_solution(12237474040930992437)
XLA Ops:
  7.2 15.5 %copy.25 = bf16[1,2,1920,256]{3,1,2,0:T(2,128)(2,1)} copy(bf16[1,2,1920,256]{3,2,1,0:T(8,128)(2,1)} %param.7) | data formatting | bytes 3932160 | tf_op args[0]
  22.7 3.4 %collective-permute-start = (bf16[2,1920,256]{2,0,1:T(2,128)(2,1)}, bf16[2,1920,256]{2,0,1:T(2,128)(2,1)S(1)}, u32[]{:S(2)}, u32[]{:S(2)}) collective-permute-start(bf16[2,1920,256]{2,0,1:T(2,128)(2,1)} %bitcast.197), channel_id=1, source_target_pairs={{4,0},{8,4},{12,8},{16,12},{20,16},{24,20},{28,24},{0,28},{5,1},{9... | collective-permute-start | bytes 5898248 | tf_op jit(solution)/shard_map/ppermute | solution.py:13
  26.1 22.4 %collective-permute-done = bf16[2,1920,256]{2,0,1:T(2,128)(2,1)S(1)} collective-permute-done((bf16[2,1920,256]{2,0,1:T(2,128)(2,1)}, bf16[2,1920,256]{2,0,1:T(2,128)(2,1)S(1)}, u32[]{:S(2)}, u32[]{:S(2)}) %collective-permute-start) | collective-permute-done | bytes 1966112 | tf_op jit(solution)/shard_map/ppermute | solution.py:13
  48.5 8.3 %gather_fusion = bf16[1920,2,256]{2,1,0:T(2,128)(2,1)} fusion(bf16[2,1920,256]{2,0,1:T(2,128)(2,1)S(1)} %collective-permute-done, s32[2048]{0:T(1024)S(1)} %pad_clamp_fusion), kind=kCustom, calls=%fused_computation | custom fusion | bytes 3939840 | tf_op jit(solution)/shard_map/gather | solution.py:52
  56.8 3.7 %broadcast_select_fusion = bf16[2,1920,256]{2,0,1:T(2,128)(2,1)S(1)} fusion(bf16[2,1920,256]{2,0,1:T(2,128)(2,1)S(1)} %collective-permute-done, pred[]{:T(512)S(6)} %eq.29, bf16[1920,2,256]{2,1,0:T(2,128)(2,1)} %gather_fusion), kind=kLoop, calls=%fused_computation.22 | loop fusion | flops 983040 | bytes 5898241 | tf_op jit(solution)/shard_map/jit(_where)/select_n | solution.py:52
  60.8 3.6 %fusion.46 = (bf16[1,1,1920,256]{3,1,2,0:T(2,128)(2,1)S(1)}, bf16[1,1,1920,256]{3,1,2,0:T(2,128)(2,1)S(1)}) fusion(bf16[1,2,1920,256]{3,1,2,0:T(2,128)(2,1)S(1)} %bitcast.228), kind=kLoop, calls=%fused_computation.108 | loop fusion | flops 491520 | bytes 3932160 | tf_op jit(solution)/shard_map/slice | solution.py:57
  68.6 40.0 %all-reduce.3.cloned.1.call-done = f32[1,2,256,256]{2,3,1,0:T(8,128)} async-done(((f32[1,2,256,256]{2,3,1,0:T(8,128)}), f32[1,2,256,256]{2,3,1,0:T(8,128)}) %all-reduce.3.cloned.1.call-update) | async-done | bytes 524304 | tf_op jit(solution)/shard_map/psum | solution.py:70
  119.5 6.3 %convolution_bitcast_fusion = f32[1,1,1024,256]{2,3,1,0:T(8,128)S(1)} fusion(bf16[3840,1024]{1,0:T(8,128)(2,1)} %bitcast.229, bf16[1,1920,256]{2,1,0:T(8,128)(2,1)S(1)} %get-tuple-element.66, bf16[1,1920,256]{2,1,0:T(8,128)(2,1)S(1)} %get-tuple-element.65), kind=kOutput, calls=%fused_computation.32 | convolution fusion | flops 2017198080 | bytes 10878976 | tf_op jit(solution)/shard_map/gp,kgn->kpn/dot_general | solution.py:38
  125.8 2.2 convolution_bitcast_fusion.1
  129.8 6.1 %convolution_bitcast_fusion.2 = f32[1,1,1024,256]{2,3,1,0:T(8,128)S(1)} fusion(bf16[3840,1024]{1,0:T(8,128)(2,1)} %bitcast.233, bf16[1,1920,256]{2,1,0:T(8,128)(2,1)} %copy-done.4, bf16[1,1920,256]{2,1,0:T(8,128)(2,1)} %copy-done.3), kind=kOutput, calls=%fused_computation.34 | convolution fusion | flops 2017198080 | bytes 10878976 | tf_op jit(solution)/shard_map/gp,kgn->kpn/dot_general | solution.py:38
  135.9 5.5 %convolution_bitcast_fusion.3 = f32[1,1,1024,256]{2,3,1,0:T(8,128)S(1)} fusion(bf16[3840,256]{1,0:T(8,128)(2,1)S(1)} %bitcast.227, bf16[3840,1024]{1,0:T(8,128)(2,1)} %bitcast.234), kind=kOutput, calls=%fused_computation.35 | convolution fusion | flops 2013265920 | bytes 10878976 | tf_op jit(solution)/shard_map/gp,kgn->kpn/dot_general | solution.py:37
  143.9 11.9 %all-gather.2.cloned.1.call-done = f32[8,2,256,256]{3,2,1,0:T(8,128)} async-done(((f32[1,2,256,256]{3,2,1,0:T(8,128)}), f32[8,2,256,256]{3,2,1,0:T(8,128)}) %all-gather.2.cloned.1.call-update) | async-done | bytes 4194320 | tf_op jit(solution)/shard_map/all_gather | solution.py:81
  155.8 61.1 %while.10 = (s32[]{:T(128)}, f32[2,256,256]{1,2,0:T(8,128)S(1)}, s32[8]{0:T(128)S(1)}, s32[]{:T(128)}, f32[8,2,256,256]{3,2,1,0:T(8,128)}, /*index=5*/s32[]{:T(128)}, s32[]{:T(128)}, s32[]{}) while((s32[]{:T(128)}, f32[2,256,256]{1,2,0:T(8,128)S(1)}, s32[8]{0:T(128)S(1)}, s32[]{:T(128)}, f32[8,2,256,256]{3,2,1,0:T(8,128)}, ...), condition=%wide.region_2.3_spmd, body=%wide.region_1.2_spmd.sunk | while | flops 805699584 | bytes 5245055 | solution.py:87
  157.3 1.6 fusion.86
  160.5 1.6 fusion.88
  163.4 1.6 fusion.85
  165.0 1.6 fusion.86
  172.7 1.6 fusion.86
  175.8 1.6 fusion.88
  178.7 1.6 fusion.85
  180.3 1.6 fusion.86
  181.9 1.6 fusion.87
  187.9 1.6 fusion.86
  195.6 1.6 fusion.86
  198.7 1.6 fusion.88
  206.3 1.6 fusion.88
  209.3 1.6 fusion.85
  210.9 1.6 fusion.86
  218.8 1.6 fusion.36
  221.6 25.2 %reduce-scatter.3.cloned.1.call-done = f32[1,2,256,256]{2,3,1,0:T(8,128)} async-done(((f32[1,2,1024,256]{2,3,1,0:T(8,128)}), f32[1,2,256,256]{2,3,1,0:T(8,128)}) %reduce-scatter.3.cloned.1.call-update) | async-done | bytes 524304 | tf_op jit(solution)/shard_map/reduce_scatter | solution.py:73
  248.3 1.6 fusion.27
  250.0 39.4 %psum.15 = f32[128]{0:T(128)} all-reduce(f32[128]{0:T(128)S(1)} %convolution_bitcast_fusion.5), channel_id=1, replica_groups=mesh['ka'=8,'ga'=4] {'ka','ga'}, use_global_device_ids=true, to_apply=%region_6.7 | all-reduce | flops 128 | bytes 1024 | tf_op jit(solution)/shard_map/psum | solution.py:98
  (102 shorter events, 57.1 us)
Async XLA Ops:
  7.2 18.9 %copy-start.5 = (s32[1920]{0:T(1024)S(1)}, s32[1920]{0:T(1024)}, u32[]{:S(2)}) copy-start(s32[1920]{0:T(1024)} %param.10) | copy-start | bytes 23044
  7.2 101.4 %all-reduce.3.cloned.1.call-start = ((), (), s32[]{:S(2)}) async-start(), calls=%async_computation.2 | async-start | bytes 1048576 | tf_op jit(solution)/shard_map/psum | solution.py:70
  22.7 25.8 %collective-permute-start = (bf16[2,1920,256]{2,0,1:T(2,128)(2,1)}, bf16[2,1920,256]{2,0,1:T(2,128)(2,1)S(1)}, u32[]{:S(2)}, u32[]{:S(2)}) collective-permute-start(bf16[2,1920,256]{2,0,1:T(2,128)(2,1)} %bitcast.197), channel_id=1, source_target_pairs={{4,0},{8,4},{12,8},{16,12},{20,16},{24,20},{28,24},{0,28},{5,1},{9... | collective-permute-start | bytes 5898248 | tf_op jit(solution)/shard_map/ppermute | solution.py:13
  64.4 1.5 copy-start
  68.3 87.5 %all-gather.2.cloned.1.call-start = ((), (), s32[]{:S(2)}) async-start(), calls=%async_computation.3 | async-start | bytes 4718592 | tf_op jit(solution)/shard_map/all_gather | solution.py:81
  108.5 4.1 %copy-start.1 = (f32[1,2,256,256]{2,3,1,0:T(8,128)S(1)}, f32[1,2,256,256]{2,3,1,0:T(8,128)}, u32[]{:S(2)}) copy-start(f32[1,2,256,256]{2,3,1,0:T(8,128)} %all-reduce.3.cloned.1.call-done) | copy-start | bytes 1572868
  119.2 99.5 %reduce-scatter.5.cloned.1.call-start = ((), (), s32[]{:S(2)}) async-start(), calls=%async_computation.5 | async-start | bytes 2621440 | tf_op jit(solution)/shard_map/reduce_scatter | solution.py:72
  119.3 6.5 %slice-start = ((s8[7864320]{0:T(1024)(128)(4,1)}), s8[4194304]{0:T(1024)(128)(4,1)S(1)}, s32[]{:S(2)}) async-start(s8[7864320]{0:T(1024)(128)(4,1)} %bitcast.230), calls=%async_computation.6 | async-start | bytes 8388608
  119.4 6.3 %copy-start.3 = (bf16[1,1920,256]{2,1,0:T(8,128)(2,1)}, bf16[1,1920,256]{2,1,0:T(8,128)(2,1)S(1)}, u32[]{:S(2)}) copy-start(bf16[1,1920,256]{2,1,0:T(8,128)(2,1)S(1)} %get-tuple-element.65) | copy-start | bytes 2949124
  119.4 6.3 %copy-start.4 = (bf16[1,1920,256]{2,1,0:T(8,128)(2,1)}, bf16[1,1920,256]{2,1,0:T(8,128)(2,1)S(1)}, u32[]{:S(2)}) copy-start(bf16[1,1920,256]{2,1,0:T(8,128)(2,1)S(1)} %get-tuple-element.66) | copy-start | bytes 2949124
  119.5 6.3 %slice-start.1 = ((s8[7864320]{0:T(1024)(128)(4,1)}), s8[3670016]{0:T(1024)(128)(4,1)S(1)}, s32[]{:S(2)}) async-start(s8[7864320]{0:T(1024)(128)(4,1)} %bitcast.230), calls=%async_computation.7 | async-start | bytes 7340032
  129.6 117.2 %reduce-scatter.3.cloned.1.call-start = ((), (), s32[]{:S(2)}) async-start(), calls=%async_computation.4 | async-start | bytes 2621440 | tf_op jit(solution)/shard_map/reduce_scatter | solution.py:73
  218.8 2.2 copy-start.2
Sparse Core Ops, SparseCore 0:
  68.4 40.1 all-reduce.2
  119.4 36.3 all-gather.1
  158.1 43.6 reduce-scatter.4
  203.9 42.8 reduce-scatter.2
where the time goes:
time: 298 us; the launch traced here: 297 us
  waiting for transfers between devices  99.5 us (33%)
  matrix products  88.6 us (30%)
  blocking collectives  39.4 us (13%)
  local copies, waits for them, and re-layouts  31.3 us (11%)
  other arithmetic  14.2 us (5%)
  between operations  14.2 us (5%)
  loops' own time  5.66 us (2%)
  starting transfers between devices  3.93 us (1%)
    psum x1, waiting for transfers between devices, local(): intersections = lax.psum(intersection_part, 'ga')  40 us
    psum x1, blocking collectives, local(): forces = lax.psum(force_part, ('ka', 'ga'))  39.4 us
    reduce_scatter x1, waiting for transfers between devices, local(): lax.psum_scatter(deriv_part, 'ga', scatter_dimension=2, tiled=True)  25.2 us
    ppermute x1, waiting for transfers between devices, from_behind(): return lax.ppermute(block, axis, route)  22.4 us
    dot_general x14, matrix products, cmul(): jnp.matmul(left_re, right_re, precision=highest)  17.3 us
    dot_general x14, matrix products, cmul(): jnp.matmul(left_im, right_im, precision=highest)  17.2 us
    unnamed x18, local copies, waits for them, and re-layouts  17 us
    dot_general x14, matrix products, cmul(): jnp.matmul(left_im, right_re, precision=highest)  16.3 us
  transfers between devices with their start and end apart: 5, of which 4 were waited for; matrix products, arithmetic and copies ran while one was open for 28% of the time, Pallas kernels for 0%

commit v1 on v0

v1 whole, which is shorter than its diff:
```python
import functools

import jax
import jax.numpy as jnp
from jax import lax
from jax.experimental import pallas as pl
from jax.experimental.pallas import tpu as pltpu
from jax.sharding import PartitionSpec as P

NA = 128
NEWTON = 2
F32 = jnp.float32
BF16 = jnp.bfloat16


def mm(left, right):
    return jnp.dot(left, right, precision=lax.Precision.HIGHEST, preferred_element_type=F32)


def cmul(lr, li, rr, ri):
    return mm(lr, rr) - mm(li, ri), mm(lr, ri) + mm(li, rr)


def kernel(
    nk, ng,
    c_hbm, p_hbm, d_hbm, map_ref, atom_ref,
    t_out, f_out,
    cv, nv, pv, lt, mp, mr, mfull, qs, scs, qr, scr, bown, tb, rb, fk, fg,
    c_sem, p_sem, sh_s, sh_r, m_s, m_r, a_s, a_r, q_s, q_r, x_s, x_r, f_s, f_r, g_s, g_r,
):
    k = lax.axis_index("ka")
    g = lax.axis_index("ga")
    rows = cv.shape[1]
    bands = cv.shape[2]
    share = pv.shape[3]
    piece = 2 * bands // ng
    even = k % 2 == 0
    odd = k % 2 == 1

    def remote(src, dst, ssem, rsem, to_k, to_g):
        return pltpu.make_async_remote_copy(
            src_ref=src, dst_ref=dst, send_sem=ssem, recv_sem=rsem,
            device_id=(to_k, to_g), device_id_type=pl.DeviceIdType.MESH,
        )

    load_c = pltpu.make_async_copy(c_hbm.at[0], cv, c_sem)
    load_c.start()

    def load(j, which):
        src = (p_hbm, d_hbm)[which]
        cols = pl.ds(pl.multiple_of(j * share, 128), share)
        return pltpu.make_async_copy(src.at[:, :, cols], pv.at[2 * j + which], p_sem.at[2 * j + which])

    for j in range(ng):
        load(j, 0).start()
        load(j, 1).start()

    barrier = pltpu.get_barrier_semaphore()
    for d in range(1, nk):
        pl.semaphore_signal(barrier, inc=1, device_id=((k + d) % nk, g), device_id_type=pl.DeviceIdType.MESH)
    for d in range(1, ng):
        pl.semaphore_signal(barrier, inc=1, device_id=(k, (g + d) % ng), device_id_type=pl.DeviceIdType.MESH)
    pl.semaphore_wait(barrier, nk + ng - 2)

    load_c.wait()
    shift = remote(cv, nv, sh_s, sh_r, (k + nk - 1) % nk, g)
    shift.start()

    def transpose_in(source):
        def body(i, carry):
            for half in range(2):
                at = pl.ds(pl.multiple_of(i * 128, 128), 128)
                block = source[half, at, :].T
                here = pl.ds(pl.multiple_of(half * rows + i * 128, 128), 128)
                there = pl.ds(pl.multiple_of((1 - half) * rows + i * 128, 128), 128)
                lt[0:bands, here] = block
                lt[bands:, there] = block if half == 1 else -block
            return carry
        lax.fori_loop(0, rows // 128, body, 0)

    transpose_in(cv)

    def m_copy(d):
        j = (g + d) % ng
        part = mp.at[pl.ds(pl.multiple_of(j * piece, 8), piece)]
        return remote(part, mr.at[g], m_s.at[d], m_r.at[g], k, j)

    def a_copy(d):
        j = (g + d) % ng
        part = mfull.at[pl.ds(pl.multiple_of(g * piece, 8), piece)]
        return remote(part, part, a_s.at[d], a_r.at[g], k, j)

    def m_partial():
        shift.wait_recv()
        mp[...] = jnp.dot(lt[...], nv[...].reshape(2 * rows, bands), preferred_element_type=F32)
        for d in range(1, ng):
            m_copy(d).start()

    def m_sum():
        own = pl.ds(pl.multiple_of(g * piece, 8), piece)
        total = mp[own]
        for d in range(1, ng):
            s = (g + d) % ng
            remote(mr.at[s], mr.at[s], m_s.at[d], m_r.at[s], k, s).wait_recv()
            total = total + mr[s]
        mfull[own] = total
        for d in range(1, ng):
            a_copy(d).start()

    def q_copies(d):
        j = (g + d) % ng
        return (
            remote(qs.at[j], qr.at[g], q_s.at[0, d], q_r.at[0, g], k, j),
            remote(scs.at[j], scr.at[g], q_s.at[1, d], q_r.at[1, g], k, j),
        )

    def q_start():
        for d in range(1, ng):
            for copy in q_copies(d):
                copy.start()

    @pl.when(even)
    def _():
        m_partial()

    def project(j, carry):
        for which in range(2):
            load(j, which).wait()
            table = pv[2 * j + which].reshape(2 * rows, share)
            res = jnp.dot(lt[...], table, preferred_element_type=F32)
            top = jnp.maximum(jnp.max(jnp.abs(res), axis=0, keepdims=True), 1e-30)
            coded = jnp.round(res * (32767.0 / top)).astype(jnp.int32)
            qs[j, which] = coded.astype(jnp.int16)
            scs[j, which] = jnp.broadcast_to(top * (1.0 / 32767.0), (8, share))

            @pl.when(j == g)
            def _():
                bown[which] = res
        return carry

    lax.fori_loop(0, ng, project, 0)

    @pl.when(even)
    def _():
        m_sum()
        q_start()

    @pl.when(k == nk - 1)
    def _():
        local = map_ref[...] % rows
        both = jnp.concatenate([cv[0], cv[1]], axis=1)

        def permute(i, carry):
            ids = lax.broadcasted_iota(jnp.int32, (128, rows), 0) + i * 128
            pick = jnp.where(ids == local, 1.0, 0.0).astype(BF16)
            moved = jnp.dot(pick, both, preferred_element_type=F32).astype(BF16)
            at = pl.ds(pl.multiple_of(i * 128, 128), 128)
            for half in range(2):
                block = moved[:, half * bands:(half + 1) * bands].T
                here = pl.ds(pl.multiple_of(half * rows + i * 128, 128), 128)
                there = pl.ds(pl.multiple_of((1 - half) * rows + i * 128, 128), 128)
                lt[0:bands, here] = block
                lt[bands:, there] = block if half == 1 else -block
            return carry

        lax.fori_loop(0, rows // 128, permute, 0)

    @pl.when(odd)
    def _():
        m_partial()
        m_sum()
        q_start()

    for d in range(1, ng):
        s = (g + d) % ng
        part = mfull.at[pl.ds(pl.multiple_of(s * piece, 8), piece)]
        remote(part, part, a_s.at[d], a_r.at[s], k, s).wait_recv()

    mre = mfull[0:bands]
    mim = -mfull[bands:]
    diagonal = lax.broadcasted_iota(jnp.int32, (bands, bands), 0) == lax.broadcasted_iota(
        jnp.int32, (bands, bands), 1
    )
    two = jnp.where(diagonal, 2.0, 0.0).astype(F32)
    xr, xi = two - mre, -mim
    for newton_step in range(NEWTON - 1):
        yr, yi = cmul(mre, mim, xr, xi)
        xr, xi = cmul(xr, xi, two - yr, -yi)
    tb[0, 0] = xr
    tb[0, 1] = xi

    step = 0
    width = 1
    while width < nk:
        now, later = tb.at[step], tb.at[step + 1]
        spot = k % (2 * width)
        is_source = spot == width - 1
        is_target = spot >= width
        if width == 1:
            copy = remote(now, rb.at[step], x_s.at[step, 0], x_r.at[step, 0], (k + 1) % nk, g)

            @pl.when(is_source)
            def _():
                copy.start()
                copy.wait_send()

            @pl.when(is_target)
            def _():
                copy.wait_recv()
        else:
            far = [
                remote(now.at[d % 2], rb.at[step, d % 2], x_s.at[step, d], x_r.at[step, 0], (k + 1 + d) % nk, g)
                for d in range(width)
            ]

            @pl.when(is_source)
            def _():
                for copy in far:
                    copy.start()

            def swap(half, partner):
                mine = rb.at[step, half]
                far[half].wait_recv()
                copy = remote(mine, mine, x_s.at[step, 0], x_r.at[step, 1], partner, g)
                copy.start()
                other = rb.at[step, 1 - half]
                remote(other, other, x_s.at[step, 0], x_r.at[step, 1], partner, g).wait_recv()
                copy.wait_send()

            @pl.when(jnp.logical_and(is_target, even))
            def _():
                swap(0, (k + 1) % nk)

            @pl.when(jnp.logical_and(is_target, odd))
            def _():
                swap(1, (k + nk - 1) % nk)

            @pl.when(is_source)
            def _():
                for copy in far:
                    copy.wait_send()

        @pl.when(is_target)
        def _():
            vr, vi = cmul(rb[step, 0], rb[step, 1], now[0], now[1])
            later[0] = vr
            later[1] = vi

        @pl.when(jnp.logical_not(is_target))
        def _():
            later[...] = now[...]

        step += 1
        width *= 2

    tr, ti = tb[step, 0], tb[step, 1]
    t_out[0, 0] = tr
    t_out[0, 1] = ti

    sums = [bown[0], bown[1]]
    for d in range(1, ng):
        s = (g + d) % ng
        remote(qr.at[s], qr.at[s], q_s.at[0, d], q_r.at[0, s], k, s).wait_recv()
        remote(scr.at[s], scr.at[s], q_s.at[1, d], q_r.at[1, s], k, s).wait_recv()
        for which in range(2):
            scale = scr[s, which][0:1]
            sums[which] = sums[which] + qr[s, which].astype(jnp.int32).astype(F32) * scale
    br, bi = sums[0][0:bands], sums[0][bands:]
    dr, di = sums[1][0:bands], sums[1][bands:]
    wr, wi = cmul(tr.T, ti.T, br, bi)
    fp = jnp.sum(dr * wi - di * wr, axis=0, keepdims=True) * (1.0 / nk)
    atoms = atom_ref[pl.ds(g, 1), :]
    onehot = (lax.broadcasted_iota(jnp.int32, (NA, share), 0) == atoms).astype(F32)
    force = lax.dot_general(
        jnp.broadcast_to(fp, (8, share)), onehot, (((1,), (1,)), ((), ())),
        precision=lax.Precision.HIGHEST, preferred_element_type=F32,
    )

    fk[pl.ds(k, 1)] = force[None]
    for d in range(1, nk):
        remote(fk.at[k], fk.at[k], f_s.at[d], f_r.at[k], (k + d) % nk, g).start()
    for d in range(1, nk):
        s = (k + d) % nk
        remote(fk.at[s], fk.at[s], f_s.at[d], f_r.at[s], s, g).wait_recv()
    total = fk[0]
    for s in range(1, nk):
        total = total + fk[s]
    fg[pl.ds(g, 1)] = total[None]
    for d in range(1, ng):
        remote(fg.at[g], fg.at[g], g_s.at[d], g_r.at[g], k, (g + d) % ng).start()
    for d in range(1, ng):
        s = (g + d) % ng
        remote(fg.at[s], fg.at[s], g_s.at[d], g_r.at[s], k, s).wait_recv()
    total = fg[0]
    for s in range(1, ng):
        total = total + fg[s]
    f_out[...] = total

    shift.wait_send()
    for d in range(1, ng):
        m_copy(d).wait_send()
        a_copy(d).wait_send()
        for copy in q_copies(d):
            copy.wait_send()
        remote(fg.at[g], fg.at[g], g_s.at[d], g_r.at[g], k, (g + d) % ng).wait_send()
    for d in range(1, nk):
        remote(fk.at[k], fk.at[k], f_s.at[d], f_r.at[k], (k + d) % nk, g).wait_send()


def local(coeffs, projectors, proj_deriv, shift_map, atom_of):
    nk, ng = lax.axis_size("ka"), lax.axis_size("ga")
    rows, bands = coeffs.shape[2:]
    count = projectors.shape[2]
    share = count // ng
    steps = max(nk - 1, 1).bit_length()
    dma = pltpu.SemaphoreType.DMA
    vm = pl.BlockSpec(memory_space=pltpu.VMEM)
    hbm = pl.BlockSpec(memory_space=pl.ANY)
    transport, forces = pl.pallas_call(
        functools.partial(kernel, nk, ng),
        out_shape=(
            jax.ShapeDtypeStruct((1, 2, bands, bands), F32),
            jax.ShapeDtypeStruct((8, NA), F32),
        ),
        in_specs=[hbm, hbm, hbm, vm, vm],
        out_specs=(vm, vm),
        scratch_shapes=[
            pltpu.VMEM((2, rows, bands), BF16),
            pltpu.VMEM((2, rows, bands), BF16),
            pltpu.VMEM((2 * ng, 2, rows, share), BF16),
            pltpu.VMEM((2 * bands, 2 * rows), BF16),
            pltpu.VMEM((2 * bands, bands), F32),
            pltpu.VMEM((ng, 2 * bands // ng, bands), F32),
            pltpu.VMEM((2 * bands, bands), F32),
            pltpu.VMEM((ng, 2, 2 * bands, share), jnp.int16),
            pltpu.VMEM((ng, 2, 8, share), F32),
            pltpu.VMEM((ng, 2, 2 * bands, share), jnp.int16),
            pltpu.VMEM((ng, 2, 8, share), F32),
            pltpu.VMEM((2, 2 * bands, share), F32),
            pltpu.VMEM((steps + 1, 2, bands, bands), F32),
            pltpu.VMEM((steps, 2, bands, bands), F32),
            pltpu.VMEM((nk, 8, NA), F32),
            pltpu.VMEM((ng, 8, NA), F32),
            dma, dma((2 * ng,)), dma, dma,
            dma((ng,)), dma((ng,)), dma((ng,)), dma((ng,)),
            dma((2, ng)), dma((2, ng)),
            dma((steps, max(nk // 2, 2))), dma((steps, 2)),
            dma((nk,)), dma((nk,)), dma((ng,)), dma((ng,)),
        ],
        compiler_params=pltpu.CompilerParams(
            collective_id=0, has_side_effects=True, vmem_limit_bytes=60 * 1024 * 1024
        ),
    )(coeffs, projectors, proj_deriv, shift_map.reshape(1, rows), atom_of.reshape(ng, share))
    return transport, forces[0]


def solution(mesh):
    placed = (P("ka", None, "ga", None), P(None, "ga", None), P(None, "ga", None), P("ga"), P())
    return jax.shard_map(
        local,
        mesh=mesh,
        in_specs=placed,
        out_specs=(P("ka", None, None, None), P()),
        check_vma=False,
    )
```

time: 298 us -> 124 us (0.42)
  Pallas kernels: 0 us -> 117 us
  waiting for transfers between devices: 99.5 us -> 0 us
  matrix products: 88.6 us -> 0 us
  blocking collectives: 39.4 us -> 0 us
  local copies, waits for them, and re-layouts: 31.3 us -> 5.63 us
  other arithmetic: 14.2 us -> 0 us
  between operations: 14.2 us -> 0.64 us
  loops' own time: 5.66 us -> 0 us
  starting transfers between devices: 3.93 us -> 0 us
    pallas_call x0 -> x1, Pallas kernels: none -> 117 us  [local(): pl.pallas_call(functools.partial(kernel, nk, ng), out_shape=(jax.ShapeDty...]
    dot_general x63 -> x0, matrix products: 88.6 us -> none  [the longest x14 17.3 us: cmul(): jnp.matmul(left_re, right_re, precision=highest)]
    psum x1 -> x0, waiting for transfers between devices: 40 us -> none  [local(): intersections = lax.psum(intersection_part, 'ga')]
    psum x1 -> x0, blocking collectives: 39.4 us -> none  [local(): forces = lax.psum(force_part, ('ka', 'ga'))]
    reduce_scatter x2 -> x0, waiting for transfers between devices: 25.2 us -> none  [the longest x1 25.2 us: local(): lax.psum_scatter(deriv_part, 'ga', scatter_dimension=2, tiled=True)]
    ppermute x1 -> x0, waiting for transfers between devices: 22.4 us -> none  [from_behind(): return lax.ppermute(block, axis, route)]
    unnamed x18 -> x1, local copies, waits for them, and re-layouts: 17 us -> 1.87 us
    all_gather x1 -> x0, waiting for transfers between devices: 11.9 us -> none  [local(): everyone = lax.all_gather(device_product[None], 'ka', axis=0, tiled=True)]
  transfers between devices with their start and end apart: 5 -> 0, of which waited for: 4 -> 0; matrix products, arithmetic and copies ran while one was open for 28% -> 0% of each run, Pallas kernels for 0% -> 0%
where the time goes in v1:
time: 124 us
  Pallas kernels  117 us (94%)
  local copies, waits for them, and re-layouts  5.63 us (5%)
    pallas_call x1, Pallas kernels, local(): pl.pallas_call(functools.partial(kernel, nk, ng), out_shape=(jax.ShapeDty...  117 us

profile of v1, /device:TPU:0, one launch (start us, length us, event | category | flops | bytes accessed | tf_op | source)
XLA Modules:
  0.0 123.7 jit_solution(5275415258657993035)
XLA Ops:
  0.6 1.3 %reshape.11.atom_ref = s32[4,256]{1,0:T(4,128)} reshape(s32[1024]{0:T(1024)} %param.9) | data formatting | bytes 8192 | tf_op jit(solution)/shard_map/reshape | solution.py:353
  1.9 1.3 %reshape.10.map_ref = s32[1,1920]{1,0:T(1,128)} reshape(s32[1920]{0:T(1024)} %param.8) | data formatting | bytes 15360 | tf_op jit(solution)/shard_map/reshape | solution.py:353
  3.2 117.4 %shard_map.68 = (f32[1,2,256,256]{3,2,1,0:T(8,128)}, f32[8,128]{1,0:T(8,128)}) custom-call(bf16[1,2,1920,256]{3,2,1,0:T(8,128)(2,1)} %c_hbm.1, bf16[2,1920,1024]{2,1,0:T(8,128)(2,1)} %p_hbm.1, bf16[2,1920,1024]{2,1,0:T(8,128)(2,1)} %d_hbm.1, s32[1,1920]{1,0:T(1,128)} %reshape.10.map_ref, s32[4,256]{1,0:T(4,128)} %reshape.11.atom_ref), custom_call_target="tpu_custom_call" | custom-call | tf_op jit(solution)/shard_map/pallas_call | solution.py:319
  120.6 1.2 slice_bitcast_fusion
  121.8 1.9 %copy.8 = f32[1,2,256,256]{3,2,1,0:T(8,128)} copy(f32[1,2,256,256]{3,2,1,0:T(8,128)} %get-tuple-element.8) | data formatting | bytes 1048576

commit v2 on v1

--- a/solution.py
+++ b/solution.py
@@ -25,8 +25,8 @@
     nk, ng,
     c_hbm, p_hbm, d_hbm, map_ref, atom_ref,
     t_out, f_out,
-    cv, nv, pv, lt, mp, mr, mfull, qs, scs, qr, scr, bown, tb, rb, fk, fg,
-    c_sem, p_sem, sh_s, sh_r, m_s, m_r, a_s, a_r, q_s, q_r, x_s, x_r, f_s, f_r, g_s, g_r,
+    cv, nv, pv, lt, mp, mr, mfull, qs, scs, qr, scr, qs2, scs2, qr2, scr2, own, tb, rb, fk, fg,
+    c_sem, p_sem, sh_s, sh_r, m_s, m_r, a_s, a_r, q_s, q_r, q2_s, q2_r, x_s, x_r, f_s, f_r, g_s, g_r,
 ):
     k = lax.axis_index("ka")
     g = lax.axis_index("ga")
@@ -36,6 +36,10 @@
     piece = 2 * bands // ng
     even = k % 2 == 0
     odd = k % 2 == 1
+    side = g % 2
+    mate = g + 1 - 2 * side
+    pair = g // 2
+    pairs = ng // 2
 
     def remote(src, dst, ssem, rsem, to_k, to_g):
         return pltpu.make_async_remote_copy(
@@ -51,9 +55,12 @@
         cols = pl.ds(pl.multiple_of(j * share, 128), share)
         return pltpu.make_async_copy(src.at[:, :, cols], pv.at[2 * j + which], p_sem.at[2 * j + which])
 
-    for j in range(ng):
-        load(j, 0).start()
-        load(j, 1).start()
+    def order(t):
+        return 2 * (t % pairs) + jnp.where(t < pairs, 1 - side, side)
+
+    for t in range(ng):
+        load(order(t), 0).start()
+        load(order(t), 1).start()
 
     barrier = pltpu.get_barrier_semaphore()
     for d in range(1, nk):
@@ -107,43 +114,77 @@
         for d in range(1, ng):
             a_copy(d).start()
 
-    def q_copies(d):
-        j = (g + d) % ng
+    def q_copies(i):
         return (
-            remote(qs.at[j], qr.at[g], q_s.at[0, d], q_r.at[0, g], k, j),
-            remote(scs.at[j], scr.at[g], q_s.at[1, d], q_r.at[1, g], k, j),
+            remote(qs.at[i], qr.at[i], q_s.at[0, i], q_r.at[0, i], k, mate),
+            remote(scs.at[i], scr.at[i], q_s.at[1, i], q_r.at[1, i], k, mate),
         )
 
-    def q_start():
-        for d in range(1, ng):
-            for copy in q_copies(d):
+    def q_start(i):
+        for copy in q_copies(i):
+            copy.start()
+
+    def q2_copies(d):
+        i = (pair + d) % pairs
+        j = 2 * i + side
+        return (
+            remote(qs2.at[i], qr2.at[pair], q2_s.at[0, i], q2_r.at[0, pair], k, j),
+            remote(scs2.at[i], scr2.at[pair], q2_s.at[1, i], q2_r.at[1, pair], k, j),
+        )
+
+    def encode(value, code_ref, scale_ref, i, which):
+        top = jnp.maximum(jnp.max(jnp.abs(value), axis=0, keepdims=True), 1e-30)
+        coded = jnp.round(value * (32767.0 / top)).astype(jnp.int32)
+        code_ref[i, which] = coded.astype(jnp.int16)
+        scale_ref[i, which] = jnp.broadcast_to(top * (1.0 / 32767.0), (8, share))
+
+    def decode(code_ref, scale_ref, i, which):
+        return code_ref[i, which].astype(jnp.int32).astype(F32) * scale_ref[i, which][0:1]
+
+    def q_arrive(i):
+        remote(qr.at[i], qr.at[i], q_s.at[0, i], q_r.at[0, i], k, mate).wait_recv()
+        remote(scr.at[i], scr.at[i], q_s.at[1, i], q_r.at[1, i], k, mate).wait_recv()
+
+    def q_second():
+        for d in range(1, pairs):
+            i = (pair + d) % pairs
+            q_arrive(i)
+            for which in range(2):
+                encode(own[i, which] + decode(qr, scr, i, which), qs2, scs2, i, which)
+            for copy in q2_copies(d):
                 copy.start()
 
     @pl.when(even)
     def _():
         m_partial()
 
-    def project(j, carry):
+    def product(j, which):
+        load(j, which).wait()
+        table = pv[2 * j + which].reshape(2 * rows, share)
+        return jnp.dot(lt[...], table, preferred_element_type=F32)
+
+    def project_mate(i, carry):
         for which in range(2):
-            load(j, which).wait()
-            table = pv[2 * j + which].reshape(2 * rows, share)
-            res = jnp.dot(lt[...], table, preferred_element_type=F32)
-            top = jnp.maximum(jnp.max(jnp.abs(res), axis=0, keepdims=True), 1e-30)
-            coded = jnp.round(res * (32767.0 / top)).astype(jnp.int32)
-            qs[j, which] = coded.astype(jnp.int16)
-            scs[j, which] = jnp.broadcast_to(top * (1.0 / 32767.0), (8, share))
-
-            @pl.when(j == g)
-            def _():
-                bown[which] = res
+            encode(product(2 * i + 1 - side, which), qs, scs, i, which)
+
+        @pl.when(odd)
+        def _():
+            q_start(i)
         return carry
 
-    lax.fori_loop(0, ng, project, 0)
+    def project_own(i, carry):
+        for which in range(2):
+            own[i, which] = product(2 * i + side, which)
+        return carry
+
+    lax.fori_loop(0, pairs, project_mate, 0)
+    lax.fori_loop(0, pairs, project_own, 0)
 
     @pl.when(even)
     def _():
         m_sum()
-        q_start()
+        for i in range(pairs):
+            q_start(i)
 
     @pl.when(k == nk - 1)
     def _():
@@ -169,7 +210,7 @@
     def _():
         m_partial()
         m_sum()
-        q_start()
+        q_second()
 
     for d in range(1, ng):
         s = (g + d) % ng
@@ -189,6 +230,12 @@
     tb[0, 0] = xr
     tb[0, 1] = xi
 
+    @pl.when(even)
+    def _():
+        if nk > 1:
+            remote(tb.at[0], rb.at[0], x_s.at[0, 0], x_r.at[0, 0], k + 1, g).start()
+        q_second()
+
     step = 0
     width = 1
     while width < nk:
@@ -201,7 +248,6 @@
 
             @pl.when(is_source)
             def _():
-                copy.start()
                 copy.wait_send()
 
             @pl.when(is_target)
@@ -257,14 +303,15 @@
     t_out[0, 0] = tr
     t_out[0, 1] = ti
 
-    sums = [bown[0], bown[1]]
-    for d in range(1, ng):
-        s = (g + d) % ng
-        remote(qr.at[s], qr.at[s], q_s.at[0, d], q_r.at[0, s], k, s).wait_recv()
-        remote(scr.at[s], scr.at[s], q_s.at[1, d], q_r.at[1, s], k, s).wait_recv()
+    q_arrive(pair)
+    sums = [own[pair, which] + decode(qr, scr, pair, which) for which in range(2)]
+    for d in range(1, pairs):
+        i = (pair + d) % pairs
+        j = 2 * i + side
+        remote(qr2.at[i], qr2.at[i], q2_s.at[0, i], q2_r.at[0, i], k, j).wait_recv()
+        remote(scr2.at[i], scr2.at[i], q2_s.at[1, i], q2_r.at[1, i], k, j).wait_recv()
         for which in range(2):
-            scale = scr[s, which][0:1]
-            sums[which] = sums[which] + qr[s, which].astype(jnp.int32).astype(F32) * scale
+            sums[which] = sums[which] + decode(qr2, scr2, i, which)
     br, bi = sums[0][0:bands], sums[0][bands:]
     dr, di = sums[1][0:bands], sums[1][bands:]
     wr, wi = cmul(tr.T, ti.T, br, bi)
@@ -297,11 +344,15 @@
     f_out[...] = total
 
     shift.wait_send()
+    for i in range(pairs):
+        for copy in q_copies(i):
+            copy.wait_send()
+    for d in range(1, pairs):
+        for copy in q2_copies(d):
+            copy.wait_send()
     for d in range(1, ng):
         m_copy(d).wait_send()
         a_copy(d).wait_send()
-        for copy in q_copies(d):
-            copy.wait_send()
         remote(fg.at[g], fg.at[g], g_s.at[d], g_r.at[g], k, (g + d) % ng).wait_send()
     for d in range(1, nk):
         remote(fk.at[k], fk.at[k], f_s.at[d], f_r.at[k], (k + d) % nk, g).wait_send()
@@ -332,18 +383,22 @@
             pltpu.VMEM((2 * bands, bands), F32),
             pltpu.VMEM((ng, 2 * bands // ng, bands), F32),
             pltpu.VMEM((2 * bands, bands), F32),
-            pltpu.VMEM((ng, 2, 2 * bands, share), jnp.int16),
-            pltpu.VMEM((ng, 2, 8, share), F32),
-            pltpu.VMEM((ng, 2, 2 * bands, share), jnp.int16),
-            pltpu.VMEM((ng, 2, 8, share), F32),
-            pltpu.VMEM((2, 2 * bands, share), F32),
+            *[
+                pltpu.VMEM(shape, kind)
+                for shape, kind in (
+                    ((ng // 2, 2, 2 * bands, share), jnp.int16),
+                    ((ng // 2, 2, 8, share), F32),
+                )
+                * 4
+            ],
+            pltpu.VMEM((ng // 2, 2, 2 * bands, share), F32),
             pltpu.VMEM((steps + 1, 2, bands, bands), F32),
             pltpu.VMEM((steps, 2, bands, bands), F32),
             pltpu.VMEM((nk, 8, NA), F32),
             pltpu.VMEM((ng, 8, NA), F32),
             dma, dma((2 * ng,)), dma, dma,
             dma((ng,)), dma((ng,)), dma((ng,)), dma((ng,)),
-            dma((2, ng)), dma((2, ng)),
+            *[dma((2, ng // 2))] * 4,
             dma((steps, max(nk // 2, 2))), dma((steps, 2)),
             dma((nk,)), dma((nk,)), dma((ng,)), dma((ng,)),
         ],

time: 124 us -> 90.6 us (0.73)
  Pallas kernels: 117 us -> 84 us
    pallas_call x1, Pallas kernels: 117 us -> 84 us  [local(): pl.pallas_call(functools.partial(kernel, nk, ng), out_shape=(jax.ShapeDty...]
where the time goes in v2:
time: 90.6 us; the launch traced here: 90.3 us
  Pallas kernels  84 us (93%)
  local copies, waits for them, and re-layouts  5.63 us (6%)
    pallas_call x1, Pallas kernels, local(): pl.pallas_call(functools.partial(kernel, nk, ng), out_shape=(jax.ShapeDty...  84 us
    unnamed x1, local copies, waits for them, and re-layouts  1.87 us

profile of v2, /device:TPU:0, one launch (start us, length us, event | category | flops | bytes accessed | tf_op | source)
XLA Modules:
  0.0 90.3 jit_solution(11895322204790199707)
XLA Ops:
  0.6 1.3 %reshape.11.atom_ref = s32[4,256]{1,0:T(4,128)} reshape(s32[1024]{0:T(1024)} %param.9) | data formatting | bytes 8192 | tf_op jit(solution)/shard_map/reshape | solution.py:408
  1.9 1.3 %reshape.10.map_ref = s32[1,1920]{1,0:T(1,128)} reshape(s32[1920]{0:T(1024)} %param.8) | data formatting | bytes 15360 | tf_op jit(solution)/shard_map/reshape | solution.py:408
  3.2 84.0 %shard_map.68 = (f32[1,2,256,256]{3,2,1,0:T(8,128)}, f32[8,128]{1,0:T(8,128)}) custom-call(bf16[1,2,1920,256]{3,2,1,0:T(8,128)(2,1)} %c_hbm.1, bf16[2,1920,1024]{2,1,0:T(8,128)(2,1)} %p_hbm.1, bf16[2,1920,1024]{2,1,0:T(8,128)(2,1)} %d_hbm.1, s32[1,1920]{1,0:T(1,128)} %reshape.10.map_ref, s32[4,256]{1,0:T(4,128)} %reshape.11.atom_ref), custom_call_target="tpu_custom_call" | custom-call | tf_op jit(solution)/shard_map/pallas_call | solution.py:370
  87.2 1.2 %slice_bitcast_fusion = f32[128]{0:T(128)} fusion(f32[8,128]{1,0:T(8,128)} %get-tuple-element.5), kind=kLoop, calls=%fused_computation | loop fusion | bytes 1024 | tf_op jit(solution)/shard_map/squeeze | solution.py:409
  88.4 1.9 %copy.8 = f32[1,2,256,256]{3,2,1,0:T(8,128)} copy(f32[1,2,256,256]{3,2,1,0:T(8,128)} %get-tuple-element.8) | data formatting | bytes 1048576
